TPU v7x, 32 devices: a whole 2x2x4 slice. The times are simulated.
32 devices in a mesh: groups: 2 (over y), sky: 4 (over z), epoch: 2 (over x), band: 2 (over core).
Axes of the slice: x: 2, y: 2, z: 4, core: 2. Of those that a mesh axis runs over, the one named last changes fastest.
Arguments:
- slot_pixels: bfloat16 [96, 6, 32, 512], P(('groups', 'sky', 'epoch'), 'band'), parts along dimension 0, may hold values from -6 to 6
- slot_tile: int32 [96, 1], P(('groups', 'sky', 'epoch')), parts along dimension 0, may hold values from 0 to 3; in each aligned block of 6 rows (0 to 5, 6 to 11, ...) at most 2 rows name the same one
- slot_offset: int32 [96, 2], P(('groups', 'sky', 'epoch')), parts along dimension 0, may hold values from -5 to 5
- slot_frac: bfloat16 [96, 2], P(('groups', 'sky', 'epoch')), parts along dimension 0, may hold values from 0.049804688 to 0.94921875
- slot_sigma: bfloat16 [96, 6], P(('groups', 'sky', 'epoch'), 'band'), parts along dimension 0, may hold values from 0.5 to 2
- clip_mask: int32 [96, 6, 16], P(('groups', 'sky', 'epoch')), parts along dimension 0, may hold values 0 or 1
- slot_count: int32 [16], P(('groups', 'sky', 'epoch')), parts along dimension 0, may hold values from 4 to 6
- template: bfloat16 [6, 256, 512], P('band', ('groups', 'sky')), parts along dimension 1, may hold values from -6 to 6
- prior_weight: float32 [6, 256], P('band', ('groups', 'sky')), parts along dimension 1, may hold values from 0.5 to 4
Outputs:
- coadd_image: bfloat16 [6, 256, 512], P('band', ('groups', 'sky'), 'epoch'), parts along dimension 1
- depth_norm: bfloat16 [6, 256, 512], P('band', ('groups', 'sky'), 'epoch'), parts along dimension 1
There are 2 independent parts, one for each index of `groups`. A program takes and returns all parts, laid end to end along the dimension named above; each array names one. Nothing has to cross between parts.
Inputs may be any that keep to these rules, and one draw needn't show every extreme that they name: `slot_tile`: among the 6 rows of one reading device no owner is named more than 2 times, a bound that some block reaches. `slot_count`: slots of a reading device at or after its count are padding.
All inputs are finite; a program needn't handle non-finite values. No bound on the sum of `clip_mask` on one device may be relied on, other than what follows from the above.
Results may differ from a plain program's by a relative error of at most 0.014.
Values may be sent and summed in bfloat16 or wider, within the bound.
A program may use at most 64 MiB of HBM per device.

v0:
```python
import functools

import jax
import jax.numpy as jnp
from jax import lax
from jax.experimental import pallas as pl
from jax.experimental.pallas import tpu as pltpu
from jax.sharding import PartitionSpec as P

MARGIN = 8
BLOCK_ROWS = 8
REACH = 3
LANES = 128
CLIP_WIDTH = 3.0
CELL_TYPE = jnp.bfloat16
MESH = pl.DeviceIdType.MESH


def lanczos(distance):
    inside = jnp.abs(distance) < 3.0
    return jnp.where(inside, jnp.sinc(distance) * jnp.sinc(distance / 3.0), 0.0)


def tap_weights(fractions):
    steps_back = jnp.arange(-REACH, REACH, dtype=jnp.int32)
    distance = (-steps_back).astype(jnp.float32)[:, None] - fractions.astype(jnp.float32)[:, None]
    rounded = lanczos(distance).astype(jnp.bfloat16)
    return lax.optimization_barrier(rounded).astype(jnp.float32)


def gather_kernel(sky, own_ref, all_ref, held, send_sem, recv_sem):
    me = lax.axis_index("sky")
    barrier = pltpu.get_barrier_semaphore()
    for d in range(1, sky):
        pl.semaphore_signal(
            barrier, inc=1, device_id={"sky": lax.rem(me + d, sky)}, device_id_type=MESH
        )
    pl.semaphore_wait(barrier, sky - 1)
    copies = []
    for d in range(1, sky):
        copy = pltpu.make_async_remote_copy(
            src_ref=own_ref,
            dst_ref=held.at[d - 1],
            send_sem=send_sem.at[d - 1],
            recv_sem=recv_sem.at[d - 1],
            device_id={"sky": lax.rem(me + d, sky)},
            device_id_type=MESH,
        )
        copy.start()
        copies.append(copy)
    all_ref[me] = own_ref[...]
    for d in range(1, sky):
        copies[d - 1].wait()
        all_ref[lax.rem(me - d + sky, sky)] = held[d - 1]


def warp_kernel(
    bands, sky, epochs, rows,
    tile_ref, offset_ref, count_ref, param_ref,
    pixels_ref, mask_ref, template_ref, prior_ref,
    send_ref, total_ref, rows_ref, cells_ref,
    framed, flux, cells, source,
):
    slots = pixels_ref.shape[0]
    cols = pixels_ref.shape[2]
    padded = cols + LANES
    canvas = rows + 2 * MARGIN
    blocks = canvas // BLOCK_ROWS
    part = cols // epochs
    mask_cols = mask_ref.shape[2]

    flux[...] = jnp.zeros_like(flux)
    cells[...] = jnp.zeros_like(cells)
    total_ref[...] = jnp.zeros_like(total_ref)
    rows_ref[...] = jnp.zeros_like(rows_ref)
    lane = lax.broadcasted_iota(jnp.int32, (sky, rows_ref.shape[2]), 1)
    patch_row = lax.broadcasted_iota(jnp.int32, lane.shape, 0) * rows + lax.rem(lane, rows)
    canvas_row = lax.broadcasted_iota(jnp.int32, (canvas, 1), 0) - MARGIN
    group = rows // BLOCK_ROWS
    first = MARGIN // BLOCK_ROWS
    edge = jnp.zeros((bands, MARGIN, cols), jnp.float32)
    framed[:, :MARGIN] = edge
    framed[:, MARGIN + sky * rows :] = edge
    for s in range(sky):
        framed[:, MARGIN + s * rows : MARGIN + (s + 1) * rows] = template_ref[s].astype(jnp.float32)
    source[:, cols:] = jnp.zeros((source.shape[0], LANES), jnp.float32)
    source[bands * rows :, :cols] = jnp.ones((8, cols), jnp.float32)
    cell = lax.broadcasted_iota(jnp.int32, (mask_cols, cols), 0)
    column = lax.broadcasted_iota(jnp.int32, (mask_cols, cols), 1) // (cols // mask_cols)
    spread = jnp.where(cell == column, 1.0, 0.0).astype(jnp.bfloat16)
    gap = (
        lax.broadcasted_iota(jnp.int32, (canvas, rows), 0)
        - lax.broadcasted_iota(jnp.int32, (canvas, rows), 1)
        - MARGIN
    )

    def one_slot(p, carry):
        dy, dx = offset_ref[0, p], offset_ref[1, p]
        source[: bands * rows, :cols] = pixels_ref[p].astype(jnp.float32)
        base = pltpu.roll(source[...], lax.rem(dx + padded, padded), 1)
        summed = param_ref[2 * REACH + REACH, p] * base
        for tap in range(2 * REACH):
            if tap != REACH:
                moved = pltpu.roll(base, (REACH - tap) % padded, 1)
                summed = summed + param_ref[2 * REACH + tap, p] * moved
        columns = summed[: bands * rows, :cols].astype(jnp.bfloat16)
        col_cover = jnp.clip(summed[bands * rows :, :cols], 0.0, 1.0)
        row_table = jnp.zeros((canvas, rows), jnp.float32)
        for tap in range(2 * REACH):
            row_table = row_table + jnp.where(gap == dy + REACH - tap, param_ref[tap, p], 0.0)
        row_cover = jnp.clip(jnp.sum(row_table, 1, keepdims=True), 0.0, 1.0)
        row_table = row_table.astype(jnp.bfloat16)
        start = pl.multiple_of(tile_ref[p] * rows, 8)
        global_row = canvas_row + start
        row_cover = jnp.where((global_row >= 0) & (global_row < sky * rows), row_cover, 0.0)
        live = jnp.where(p < count_ref[0], 1.0, 0.0)
        wide_mask = live * jnp.dot(
            mask_ref[p].astype(jnp.bfloat16), spread, preferred_element_type=jnp.float32
        )
        pieces = []
        for i in range(blocks):
            cover = row_cover[i * BLOCK_ROWS : (i + 1) * BLOCK_ROWS]
            cell_row = wide_mask[i : i + 1] * col_cover[:1]
            cells[tile_ref[p] * group + i, pl.ds(p, 1)] = cell_row
            pieces.append(cell_row * cover)
        plane = jnp.concatenate(pieces, 0)
        tile_row = patch_row - start - dy
        profile = jnp.zeros(lane.shape, jnp.float32)
        for tap in range(2 * REACH):
            from_row = tile_row + (tap - REACH)
            profile = profile + jnp.where((from_row >= 0) & (from_row < rows), param_ref[tap, p], 0.0)
        profile = jnp.clip(profile, 0.0, 1.0)
        inverse = jnp.zeros(lane.shape, jnp.float32)
        along = jnp.sum(plane, 0, keepdims=True)
        folded = along[:, :LANES]
        for c in range(1, cols // LANES):
            folded = folded + along[:, c * LANES : (c + 1) * LANES]
        for b in range(bands):
            inverse = jnp.where(lane // rows == b, param_ref[4 * REACH + 2 * bands + b, p], inverse)
            total_ref[b : b + 1] += folded * param_ref[4 * REACH + 2 * bands + b, p]
        profile = profile * inverse
        for s in range(sky):
            rows_ref[s, pl.ds(p, 1)] = profile[s : s + 1]
        for b in range(bands):
            warped = jnp.dot(
                row_table, columns[b * rows : (b + 1) * rows], preferred_element_type=jnp.float32
            )
            frame = framed[b, pl.ds(start, canvas)]
            scale = param_ref[4 * REACH + b, p]
            clipped = frame + scale * jnp.tanh((warped - frame) * param_ref[4 * REACH + bands + b, p])
            weight = plane * param_ref[4 * REACH + 2 * bands + b, p]
            flux[b, pl.ds(start, canvas)] += weight * clipped
        return carry

    lax.fori_loop(0, slots, one_slot, 0)
    for s in range(sky):
        near = slice(MARGIN + s * rows, MARGIN + (s + 1) * rows)
        for e in range(epochs):
            far = slice(e * part, (e + 1) * part)
            send_ref[s * epochs + e] = flux[:, near, far].astype(jnp.bfloat16)
            for g in range(group):
                cells_ref[s * epochs + e, g] = cells[first + s * group + g, :, far].astype(CELL_TYPE)
    for b in range(bands):
        prior = jnp.sum(prior_ref[b : b + 1], 1, keepdims=True)
        total_ref[b : b + 1] += prior * (part / LANES)


def exchange_kernel(
    bands, sky, epochs, pixels_all,
    send_ref, total_ref, rows_ref, cells_ref, template_ref, prior_ref,
    coadd_ref, depth_ref,
    held, held_total, held_rows, held_cells, send_sem, recv_sem,
):
    count = sky * epochs
    part = coadd_ref.shape[2]
    epoch = lax.axis_index("epoch")
    me = lax.axis_index("sky") * epochs + epoch

    def peer(d):
        index = lax.rem(me + d, count)
        return index, {"sky": index // epochs, "epoch": lax.rem(index, epochs)}

    barrier = pltpu.get_barrier_semaphore()
    for d in range(1, count):
        pl.semaphore_signal(barrier, inc=1, device_id=peer(d)[1], device_id_type=MESH)
    pl.semaphore_wait(barrier, count - 1)
    copies = []
    for large in (False, True):
        for d in range(1, count):
            index, where = peer(d)
            moves = (
                (send_ref.at[index], held),
                (total_ref, held_total),
                (rows_ref.at[index // epochs], held_rows),
                (cells_ref.at[index], held_cells),
            )
            for k, (src, dst) in enumerate(moves):
                if large == (k == 0):
                    copy = pltpu.make_async_remote_copy(
                        src_ref=src,
                        dst_ref=dst.at[d - 1],
                        send_sem=send_sem.at[k, d - 1],
                        recv_sem=recv_sem.at[k, d - 1],
                        device_id=where,
                        device_id_type=MESH,
                    )
                    copy.start()
                    copies.append(copy)
    for copy in copies[: 1 - count]:
        copy.wait()
    total = total_ref[...]
    for d in range(1, count):
        total = total + held_total[d - 1]
    mean = jnp.sum(total, 1, keepdims=True) * (1.0 / pixels_all)
    rows = template_ref.shape[1]
    group = rows // BLOCK_ROWS
    diagonal = lax.broadcasted_iota(jnp.int32, (rows, rows), 0) == lax.broadcasted_iota(
        jnp.int32, (rows, rows), 1
    )
    sky_me = lax.axis_index("sky")

    def weight_from(profile, cell):
        block = lax.broadcasted_iota(jnp.int32, profile.shape, 1) // BLOCK_ROWS
        block = lax.rem(block, group)
        wide = [jnp.where(block == g, profile, 0.0) for g in range(group)]
        wide = jnp.concatenate(wide, 0).astype(jnp.bfloat16)
        cell = jnp.concatenate([cell[g].astype(jnp.float32) for g in range(group)], 0)
        return lax.dot_general(
            wide, cell.astype(jnp.bfloat16), (((0,), (0,)), ((), ())),
            preferred_element_type=jnp.float32,
        )

    weights = weight_from(rows_ref[sky_me], cells_ref[me])
    for d in range(1, count):
        weights = weights + weight_from(held_rows[d - 1], held_cells[d - 1])
    for copy in copies[1 - count :]:
        copy.wait()
    for b in range(bands):
        flux = send_ref[me, b].astype(jnp.float32)
        weight = weights[b * rows : (b + 1) * rows]
        for d in range(1, count):
            flux = flux + held[d - 1, b].astype(jnp.float32)
        prior = jnp.sum(jnp.where(diagonal, prior_ref[b : b + 1], 0.0), 1, keepdims=True)
        columns = pl.ds(pl.multiple_of(epoch * part, LANES), part)
        template = template_ref[b, :, columns].astype(jnp.float32)
        depth = weight + prior
        coadd_ref[b] = ((flux + prior * template) / depth).astype(jnp.bfloat16)
        depth_ref[b] = (depth / mean[b : b + 1]).astype(jnp.bfloat16)


def on_device(
    slot_pixels, slot_tile, slot_offset, slot_frac, slot_sigma, clip_mask, slot_count, template, prior_weight
):
    sky = lax.axis_size("sky")
    epochs = lax.axis_size("epoch")
    count = sky * epochs
    slots, bands, rows, cols = slot_pixels.shape
    canvas = rows + 2 * MARGIN
    part = cols // epochs
    vmem = pl.BlockSpec(memory_space=pltpu.VMEM)
    smem = pl.BlockSpec(memory_space=pltpu.SMEM)
    templates = pl.pallas_call(
        functools.partial(gather_kernel, sky),
        out_shape=jax.ShapeDtypeStruct((sky,) + template.shape, jnp.bfloat16),
        in_specs=[vmem],
        out_specs=vmem,
        scratch_shapes=[
            pltpu.VMEM((sky - 1,) + template.shape, jnp.bfloat16),
            pltpu.SemaphoreType.DMA((sky - 1,)),
            pltpu.SemaphoreType.DMA((sky - 1,)),
        ],
        compiler_params=pltpu.CompilerParams(collective_id=0, has_side_effects=True),
        name="gather_templates",
    )(template)
    taps = tap_weights(slot_frac.T).reshape(4 * REACH, slots)
    sigma = slot_sigma.T.astype(jnp.float32)
    scale = CLIP_WIDTH * sigma
    params = jnp.concatenate([taps, scale, 1.0 / scale, 1.0 / (sigma * sigma)], 0)
    patch = sky * rows + 2 * MARGIN
    sums = pltpu.VMEM((bands, patch, cols), jnp.float32)
    held_slots = slots + -slots % 8
    lanes = bands * rows + -(bands * rows) % LANES
    group = rows // BLOCK_ROWS
    patch_blocks = sky * group + 2 * MARGIN // BLOCK_ROWS
    send, total, row_factor, cell_factor = pl.pallas_call(
        functools.partial(warp_kernel, bands, sky, epochs, rows),
        out_shape=(
            jax.ShapeDtypeStruct((count, bands, rows, part), jnp.bfloat16),
            jax.ShapeDtypeStruct((8 * -(-bands // 8), LANES), jnp.float32),
            jax.ShapeDtypeStruct((sky, held_slots, lanes), jnp.float32),
            jax.ShapeDtypeStruct((count, group, held_slots, part), CELL_TYPE),
        ),
        in_specs=[smem] * 4 + [vmem] * 4,
        out_specs=(vmem,) * 4,
        scratch_shapes=[
            sums,
            sums,
            pltpu.VMEM((patch_blocks, held_slots, cols), jnp.float32),
            pltpu.VMEM((bands * rows + 8, cols + LANES), jnp.float32),
        ],
        name="warp_slots",
    )(
        slot_tile[:, 0], slot_offset.T, slot_count, params,
        slot_pixels.reshape(slots, bands * rows, cols), clip_mask, templates, prior_weight,
    )
    block = jax.ShapeDtypeStruct((bands, rows, part), jnp.bfloat16)
    return pl.pallas_call(
        functools.partial(exchange_kernel, bands, sky, epochs, sky * rows * cols),
        out_shape=(block, block),
        in_specs=[vmem] * 6,
        out_specs=(vmem, vmem),
        scratch_shapes=[
            pltpu.VMEM((count - 1,) + send.shape[1:], jnp.bfloat16),
            pltpu.VMEM((count - 1,) + total.shape, jnp.float32),
            pltpu.VMEM((count - 1,) + row_factor.shape[1:], jnp.float32),
            pltpu.VMEM((count - 1,) + cell_factor.shape[1:], CELL_TYPE),
            pltpu.SemaphoreType.DMA((4, count - 1)),
            pltpu.SemaphoreType.DMA((4, count - 1)),
        ],
        compiler_params=pltpu.CompilerParams(collective_id=1, has_side_effects=True),
        name="exchange_sums",
    )(send, total, row_factor, cell_factor, template, prior_weight)


def solution(mesh):
    in_specs = (
        P(("groups", "sky", "epoch"), "band", None, None),
        P(("groups", "sky", "epoch"), None),
        P(("groups", "sky", "epoch"), None),
        P(("groups", "sky", "epoch"), None),
        P(("groups", "sky", "epoch"), "band"),
        P(("groups", "sky", "epoch"), None, None),
        P(("groups", "sky", "epoch")),
        P("band", ("groups", "sky"), None),
        P("band", ("groups", "sky")),
    )
    out_specs = (P("band", ("groups", "sky"), "epoch"), P("band", ("groups", "sky"), "epoch"))
    return jax.shard_map(
        on_device, mesh=mesh, in_specs=in_specs, out_specs=out_specs, check_vma=False
    )
```

profile of v0, /device:TPU:0, one launch (start us, length us, event | category | flops | bytes accessed | tf_op | source)
XLA Modules:
  0.0 44.7 jit_solution(17231774916691696777)
XLA Ops:
  1.3 0.0 copy-start.2
  1.3 0.6 %copy-done.2 = bf16[6,2]{0,1:T(2,128)(2,1)S(1)} copy-done((bf16[6,2]{0,1:T(2,128)(2,1)S(1)}, bf16[6,2]{0,1:T(2,128)(2,1)}, u32[]{:S(2)}) %copy-start.2) | copy-done | bytes 48
  1.9 0.0 copy-start.1
  1.9 0.7 %copy-done.1 = bf16[6,3]{0,1:T(4,128)(2,1)S(1)} copy-done((bf16[6,3]{0,1:T(4,128)(2,1)S(1)}, bf16[6,3]{0,1:T(4,128)(2,1)}, u32[]{:S(2)}) %copy-start.1) | copy-done | bytes 60
  2.6 0.1 copy.14
  2.7 0.1 copy.13
  2.8 0.1 fusion.16
  3.0 0.1 reshape.24
  3.0 0.1 pad_maximum_fusion
  3.1 0.7 %copy.15.param_ref = f32[21,6]{1,0:T(8,128)} copy(f32[21,6]{0,1:T(8,128)S(1)} %pad_maximum_fusion) | data formatting | bytes 1008 | tf_op jit(solution)/shard_map/concatenate | solution.py:278
  3.8 14.1 %gather_templates.1.template_ref = bf16[4,3,32,512]{3,2,1,0:T(8,128)(2,1)} custom-call(bf16[3,32,512]{2,1,0:T(8,128)(2,1)} %template_ref.1), custom_call_target="tpu_custom_call" | custom-call | tf_op jit(solution)/shard_map/gather_templates/pallas_call | solution.py:262
  17.9 6.3 %warp_slots.1 = (bf16[8,3,32,256]{3,2,1,0:T(8,128)(2,1)}, f32[8,128]{1,0:T(8,128)}, f32[4,8,128]{2,1,0:T(8,128)}, bf16[8,4,8,256]{3,2,1,0:T(8,128)(2,1)}) custom-call(s32[6]{0:T(128)} %bitcast.15, s32[2,6]{1,0:T(2,128)} %bitcast.14, s32[1]{0:T(128)S(6)} %copy.18.count_ref, f32[21,6]{1,0:T(8,128)} %copy.15.param_ref, bf16[6,96,512]{2,1,0:T(8,128)(2,1)} %bitcast.13, ...), custom_call_target="tpu_custom_call" | custom-call | tf_op jit(solution)/shard_map/warp_slots/pallas_call | solution.py:285
  24.2 18.4 %exchange_sums.1 = (bf16[3,32,256]{2,1,0:T(8,128)(2,1)}, bf16[3,32,256]{2,1,0:T(8,128)(2,1)}) custom-call(bf16[8,3,32,256]{3,2,1,0:T(8,128)(2,1)} %get-tuple-element.7.send_ref, f32[8,128]{1,0:T(8,128)} %get-tuple-element.8.total_ref, f32[4,8,128]{2,1,0:T(8,128)} %get-tuple-element.9.rows_ref, bf16[8,4,8,256]{3,2,1,0:T(8,128)(2,1)} %get-tuple-element.10.cells_ref, ...), custom_call_target="tpu_custom_call" | custom-call | tf_op jit(solution)/shard_map/exchange_sums/pallas_call | solution.py:307
  42.6 0.0 copy-start
  42.6 1.4 %copy.19 = bf16[3,32,256]{2,1,0:T(8,128)(2,1)} copy(bf16[3,32,256]{2,1,0:T(8,128)(2,1)} %get-tuple-element.15) | data formatting | bytes 98304
  44.1 0.0 copy-done
  44.1 0.6 %copy.20 = bf16[3,32,256]{2,1,0:T(8,128)(2,1)} copy(bf16[3,32,256]{2,1,0:T(8,128)(2,1)S(1)} %copy-done) | data formatting | bytes 98304
  (4 shorter events, 0.0 us)
Async XLA Ops:
  1.3 0.7 %copy-start.2 = (bf16[6,2]{0,1:T(2,128)(2,1)S(1)}, bf16[6,2]{0,1:T(2,128)(2,1)}, u32[]{:S(2)}) copy-start(bf16[6,2]{0,1:T(2,128)(2,1)} %param.13) | copy-start | bytes 76
  1.9 0.7 %copy-start.1 = (bf16[6,3]{0,1:T(4,128)(2,1)S(1)}, bf16[6,3]{0,1:T(4,128)(2,1)}, u32[]{:S(2)}) copy-start(bf16[6,3]{0,1:T(4,128)(2,1)} %param.14) | copy-start | bytes 112
  42.6 1.4 %copy-start = (bf16[3,32,256]{2,1,0:T(8,128)(2,1)S(1)}, bf16[3,32,256]{2,1,0:T(8,128)(2,1)}, u32[]{:S(2)}) copy-start(bf16[3,32,256]{2,1,0:T(8,128)(2,1)} %get-tuple-element.16) | copy-start | bytes 147460
where the time goes:
time: 45 us; the launch traced here: 44.7 us
  Pallas kernels  38.8 us (86%)
  local copies, waits for them, and re-layouts  4.35 us (10%)
  between operations  1.32 us (3%)
    pallas_call x1, Pallas kernels, on_device(): pl.pallas_call(functools.partial(exchange_kernel, bands, sky, epochs, sky...  18.4 us
    pallas_call x1, Pallas kernels, on_device(): pl.pallas_call(functools.partial(gather_kernel, sky), out_shape=jax.Shape...  14.1 us
    pallas_call x1, Pallas kernels, on_device(): pl.pallas_call(functools.partial(warp_kernel, bands, sky, epochs, rows),...  6.35 us
    unnamed x9, local copies, waits for them, and re-layouts  3.48 us

commit v1 on v0

v1 whole, which is shorter than its diff:
```python
import functools
import math

import jax
import jax.numpy as jnp
from jax import lax
from jax.experimental import pallas as pl
from jax.experimental.pallas import tpu as pltpu
from jax.sharding import PartitionSpec as P

MARGIN = 8
BLOCK_ROWS = 8
REACH = 3
TAPS = 2 * REACH
LANES = 128
CAPACITY = 2
CLIP_WIDTH = 3.0
NOBODY = -64.0
PRIOR_LANE = 64
AT_ONCE = 4
TILE, DY, DX, FY, FX, SIGMA = range(6)
MESH = pl.DeviceIdType.MESH
F32 = jnp.float32
BF16 = jnp.bfloat16


def sinc(x):
    at_zero = x == 0.0
    turned = math.pi * jnp.where(at_zero, 1.0, x)
    return jnp.where(at_zero, 1.0, jnp.sin(turned) / turned)


def lanczos(distance):
    inside = jnp.abs(distance) < 3.0
    return jnp.where(inside, sinc(distance) * sinc(distance / 3.0), 0.0)


def rounded(x):
    return x.astype(BF16).astype(F32)


def iota(shape, dim):
    return lax.broadcasted_iota(jnp.int32, shape, dim)


def ones_where(condition):
    return jnp.where(condition, 1.0, 0.0).astype(BF16)


def dot(a, b):
    return jnp.dot(a, b, preferred_element_type=F32)


def dot_first(a, b):
    return lax.dot_general(a, b, (((0,), (0,)), ((), ())), preferred_element_type=F32)


def between(x, extent):
    return (x >= 0.0) & (x < float(extent))


def coadd_kernel(
    shape, steer_ref, count_ref, tile_ref, offset_ref, frac_ref, sigma_ref, mask_ref,
    template_ref, prior_ref, pixels_ref,
    coadd_ref, depth_ref,
    pixels, small, group, others, tap_table, columns, columns_held, template_held,
    framed, flux, left, weigh, inverse, warped, send, held, cover_ref,
    local_sem, group_sem, others_sem, template_sem, columns_sem, flux_sem,
):
    bands, sky, epochs, rows, cols, slots, blocks, mask_cols = shape
    part = cols // epochs
    canvas = rows + 2 * MARGIN
    padded = cols + LANES
    held_slots = slots + -slots % 8
    fields = SIGMA + bands
    field_at = blocks * mask_cols
    at_once = sky if sky <= AT_ONCE else 1
    pairs = at_once * CAPACITY
    me = lax.axis_index("sky")
    epoch = lax.axis_index("epoch")
    own_cols = pl.ds(pl.multiple_of(epoch * part, LANES), part)

    def sky_peer(d):
        return lax.rem(me + d, sky)

    def epoch_peer(d):
        return lax.rem(epoch + d, epochs)

    barrier = pltpu.get_barrier_semaphore()
    for d in range(1, sky):
        pl.semaphore_signal(barrier, inc=1, device_id={"sky": sky_peer(d)}, device_id_type=MESH)
    for d in range(1, epochs):
        pl.semaphore_signal(barrier, inc=1, device_id={"epoch": epoch_peer(d)}, device_id_type=MESH)
    loads = []
    for b in range(bands):
        load = pltpu.make_async_copy(pixels_ref.at[:, b], pixels.at[b], local_sem.at[b])
        load.start()
        loads.append(load)

    def remote(src, dst, sems, index, where):
        copy = pltpu.make_async_remote_copy(
            src_ref=src, dst_ref=dst, send_sem=sems.at[(0,) + index], recv_sem=sems.at[(1,) + index],
            device_id=where, device_id_type=MESH,
        )
        copy.start()
        return copy

    lane = iota((8, LANES), 1)
    small[...] = jnp.ones_like(small)
    tile = jnp.where(iota((1, slots), 1) < count_ref[0], tile_ref[...].astype(F32), NOBODY)
    small[TILE : TILE + 1] = jnp.full((1, LANES), NOBODY, F32)
    small[TILE : TILE + 1, :slots] = tile
    small[DY : DX + 1, :slots] = offset_ref[...].astype(F32)
    small[FY : FX + 1, :slots] = frac_ref[...].astype(F32)
    small[SIGMA:fields, :slots] = sigma_ref[...].astype(F32)
    by_lane = small[...]
    field_rows = by_lane.shape[0]
    place = ones_where(iota((16, LANES), 1) == iota((16, LANES), 0) + field_at)
    tall = jnp.concatenate([by_lane, jnp.zeros((16 - field_rows, LANES), F32)], 0) if field_rows < 16 else by_lane
    by_slot = dot_first(tall.astype(BF16), place[: tall.shape[0]])[:held_slots]
    cells = []
    for p in range(held_slots):
        if p < slots:
            cells.append(mask_ref[p].astype(F32))
            if blocks % 8:
                cells.append(jnp.zeros((-blocks % 8, mask_cols), F32))
        else:
            cells.append(jnp.zeros((blocks + -blocks % 8, mask_cols), F32))
    cells = jnp.concatenate(cells, 0)
    tall_blocks = blocks + -blocks % 8
    wide = (mask_cols, LANES)
    spread = ones_where((lax.rem(iota(wide, 1), mask_cols) == iota(wide, 0)) & (iota(wide, 1) < field_at))
    wide = dot(cells.astype(BF16), spread)
    wide = jnp.where(iota(wide.shape, 1) // mask_cols == lax.rem(iota(wide.shape, 0), tall_blocks), wide, 0.0)
    gather = (held_slots, held_slots * tall_blocks)
    by_slot = by_slot + dot(ones_where(iota(gather, 1) // tall_blocks == iota(gather, 0)), wide.astype(BF16))
    prior = jnp.concatenate([prior_ref[...], jnp.zeros((-bands % 8, rows), F32)], 0)
    prior = jnp.sum(prior, 1, keepdims=True)
    high = rounded(prior)
    middle = rounded(prior - high)
    by_lane = jnp.where(lane == PRIOR_LANE, high, by_lane)
    by_lane = jnp.where(lane == PRIOR_LANE + 1, middle, by_lane)
    by_lane = jnp.where(lane == PRIOR_LANE + 2, prior - high - middle, by_lane)
    group[0] = jnp.concatenate([by_slot, by_lane], 0).astype(BF16)

    def column(a, f):
        return a[:, field_at + f : field_at + f + 1]

    def slot_taps(a):
        at = iota(a.shape, 1)
        fraction = jnp.where(at < 8, column(a, FX), column(a, FY))
        return rounded(lanczos((REACH - lax.rem(at, 8)).astype(F32) - fraction))

    def column_cover(a, taps, first, width):
        at = (iota((a.shape[0], width), 1) + first).astype(F32) - column(a, DX)
        total = jnp.zeros(at.shape, F32)
        for t in range(TAPS):
            total = total + jnp.where(between(at + float(t - REACH), cols), taps[:, t : t + 1], 0.0)
        return jnp.clip(total, 0.0, 1.0)

    taps = slot_taps(by_slot)
    for t in range(TAPS):
        tap_table[t] = jnp.broadcast_to(taps[:, t : t + 1], (held_slots, LANES))

    def warp_columns(b):
        def one_slot(p, carry):
            source = jnp.concatenate([pixels[b, p].astype(F32), jnp.zeros((rows, LANES), F32)], 1)
            base = pltpu.roll(source, lax.rem(steer_ref[1, p] + padded, padded), 1)

            def tap(t):
                return jnp.concatenate([tap_table[t, pl.ds(p, 1)]] * (padded // LANES), 1)

            summed = tap(REACH) * base
            for t in range(TAPS):
                if t != REACH:
                    summed = summed + tap(t) * pltpu.roll(base, (REACH - t) % padded, 1)
            at = pl.ds(pl.multiple_of(p * rows, rows), rows)
            for e in range(epochs):
                columns[e, b, at] = summed[:, e * part : (e + 1) * part].astype(BF16)
            return carry

        lax.fori_loop(0, slots, one_slot, 0, unroll=slots <= 8)

    started = []
    columns_copies, template_copies, group_copies, others_copies, flux_copies = {}, {}, {}, {}, {}
    for b in range(bands):
        loads[b].wait()
        warp_columns(b)
        if b == 0:
            pl.semaphore_wait(barrier, sky - 1 + epochs - 1)
            for d in range(1, epochs):
                group_copies[d] = remote(
                    group.at[0], group.at[d], group_sem, (d - 1,), {"epoch": epoch_peer(d)}
                )
        for d in range(1, sky):
            template_copies[d, b] = remote(
                template_ref.at[b, :, own_cols], template_held.at[d - 1, b], template_sem, (d - 1, b),
                {"sky": sky_peer(d)},
            )
        for d in range(1, epochs):
            columns_copies[d, b] = remote(
                columns.at[epoch_peer(d), b], columns_held.at[d - 1, b], columns_sem, (d - 1, b),
                {"epoch": epoch_peer(d)},
            )

    flux[...] = jnp.zeros_like(flux)
    edge = jnp.zeros((bands, MARGIN, part), F32)
    framed[:, :MARGIN] = edge
    framed[:, MARGIN + sky * rows :] = edge
    own_rows = pl.ds(pl.multiple_of(MARGIN + me * rows, 8), rows)
    for b in range(bands):
        framed[b, own_rows] = template_ref[b, :, own_cols].astype(F32)

    depth_k = slots * rows
    cell_k = blocks * held_slots
    to_rows = ones_where(iota((LANES, depth_k), 1) // rows == iota((LANES, depth_k), 0))
    to_cells = (LANES, cell_k)
    to_cells = ones_where(
        (lax.rem(iota(to_cells, 1), held_slots) == iota(to_cells, 0)) & (iota(to_cells, 0) < slots)
    )

    def prepare(d, first_owner):
        message = group[d].astype(F32)
        a, by_lane = message[:held_slots], message[held_slots:]
        lanes = iota((held_slots, LANES), 1)
        same = (column(a, TILE) == by_lane[TILE : TILE + 1]) & (iota(lanes.shape, 0) < lanes)
        rank = jnp.sum(jnp.where(same, 1.0, 0.0), 0, keepdims=True)
        tap_rows = (REACH - iota((8, LANES), 0)).astype(F32) - by_lane[FY : FY + 1]
        tap_rows = rounded(lanczos(tap_rows))
        stack = jnp.concatenate(
            [tap_rows, jnp.broadcast_to(rank, (8, LANES)), by_lane] + [tap_rows] * (by_lane.shape[0] // 8 % 2), 0
        ).astype(BF16)
        k_stack = dot(stack, to_rows)
        gap = iota((canvas, depth_k), 0) - MARGIN - lax.rem(iota((canvas, depth_k), 1), rows)
        gap = gap.astype(F32) - k_stack[16 + DY : 17 + DY]
        row_table = jnp.zeros((canvas, depth_k), F32)
        for t in range(TAPS):
            row_table = row_table + jnp.where(gap == float(REACH - t), k_stack[t : t + 1], 0.0)
        c_stack = dot(stack, to_cells)
        c_lane = iota((canvas, cell_k), 1)
        reach = (iota((canvas, cell_k), 0) - MARGIN).astype(F32) - c_stack[16 + DY : 17 + DY]
        cover = jnp.zeros((canvas, cell_k), F32)
        for t in range(TAPS):
            cover = cover + jnp.where(between(reach + float(t - REACH), rows), c_stack[t : t + 1], 0.0)
        cover = jnp.clip(cover, 0.0, 1.0)
        cover = jnp.where(iota((canvas, cell_k), 0) // BLOCK_ROWS == c_lane // held_slots, cover, 0.0)
        cover = jnp.where(lax.rem(c_lane, held_slots) < slots, cover, 0.0)
        slot_cover = column_cover(a, slot_taps(a), epoch * part, part)
        chosen = [jnp.where(iota(a.shape, 1) // mask_cols == i, a, 0.0) for i in range(blocks)]
        wide = (LANES, part)
        spread = lax.rem(iota(wide, 0), mask_cols) == (iota(wide, 1) + epoch * part) // (cols // mask_cols)
        spread = ones_where(spread & (iota(wide, 0) < field_at))
        cells = dot(jnp.concatenate(chosen, 0).astype(BF16), spread)
        cells = (cells * jnp.concatenate([slot_cover] * blocks, 0)).astype(BF16)

        def here(stacked, owner, k):
            return (stacked[16 + TILE : 17 + TILE] == owner.astype(F32)) & (stacked[8:9] == float(k))

        pair_row = iota((pairs, LANES), 0)
        picked = (by_lane[TILE : TILE + 1] == (first_owner + pair_row // CAPACITY).astype(F32)) & (
            rank == lax.rem(pair_row, CAPACITY).astype(F32)
        ) & (iota((pairs, LANES), 1) < slots)
        for b in range(bands):
            scale = 1.0 / (CLIP_WIDTH * by_lane[SIGMA + b : SIGMA + b + 1])
            scale = jnp.sum(jnp.where(picked, scale, 0.0), 1, keepdims=True)
            inverse[d, b] = jnp.broadcast_to(scale, (pairs, LANES))
        sigma = [c_stack[16 + SIGMA + b : 17 + SIGMA + b] for b in range(bands)]
        weight = [cover * (CLIP_WIDTH / jnp.where(s > 0.0, s, 1.0)) for s in sigma]
        lhs = [[] for _ in range(bands)]
        for pair in range(pairs):
            owner, k = jnp.int32(first_owner + pair // CAPACITY), pair % CAPACITY
            at = slice(pair * canvas, (pair + 1) * canvas)
            left[d, at] = jnp.where(here(k_stack, owner, k), row_table, 0.0).astype(BF16)
            mine = here(c_stack, owner, k)
            for b in range(bands):
                lhs[b].append(jnp.where(mine, weight[b], 0.0))
        for b in range(bands):
            weigh[d, b] = dot(jnp.concatenate(lhs[b], 0).astype(BF16), cells)

    def process(d, b, first_owner):
        source = columns[epoch, b] if d == 0 else columns_held[d - 1, b]
        warped[...] = dot(left[d], source)
        for o in range(at_once):
            at = pl.ds(pl.multiple_of((first_owner + o) * rows, 8), canvas)
            frame = framed[b, at]
            total = flux[b, at]
            for k in range(CAPACITY):
                pair = o * CAPACITY + k
                here = slice(pair * canvas, (pair + 1) * canvas)
                scale = jnp.concatenate([inverse[d, b, pair : pair + 1]] * (part // LANES), 1)
                total = total + weigh[d, b, here] * jnp.tanh((warped[here] - frame) * scale)
            flux[b, at] = total

    def all_owners(step):
        if sky == at_once:
            step(0)
        else:
            lax.fori_loop(0, sky // at_once, lambda i, c: (step(i * at_once), c)[1], 0)

    for d in range(1, epochs):
        group_copies[d].wait_recv()
    for d in range(1, sky):
        others_copies[d] = remote(group, others.at[d - 1], others_sem, (d - 1,), {"sky": sky_peer(d)})
    if sky == at_once:
        for d in range(epochs):
            prepare(d, 0)
    for b in range(bands):
        for d in range(1, sky):
            template_copies[d, b].wait_recv()
            at = pl.ds(pl.multiple_of(MARGIN + lax.rem(me - d + sky, sky) * rows, 8), rows)
            framed[b, at] = template_held[d - 1, b].astype(F32)
        for d in range(epochs):
            if d:
                columns_copies[d, b].wait_recv()

            def step(first_owner, d=d, b=b):
                if sky != at_once:
                    prepare(d, first_owner)
                process(d, b, first_owner)

            all_owners(step)
        for d in range(1, sky):
            at = pl.ds(pl.multiple_of(MARGIN + sky_peer(d) * rows, 8), rows)
            send[d - 1, b] = flux[b, at].astype(BF16)
            flux_copies[d, b] = remote(
                send.at[d - 1, b], held.at[d - 1, b], flux_sem, (d - 1, b), {"sky": sky_peer(d)}
            )

    for d in range(1, sky):
        others_copies[d].wait_recv()
    square = (LANES, LANES)
    by_block = iota(square, 0) // BLOCK_ROWS == iota(square, 1) // mask_cols
    by_block = ones_where(by_block & (iota(square, 0) < canvas) & (iota(square, 1) < field_at))
    wide = (cols, LANES)
    by_cell = ones_where(iota(wide, 0) // (cols // mask_cols) == lax.rem(iota(wide, 1), mask_cols))
    wide = (LANES, part)
    to_cols = lax.rem(iota(wide, 0), mask_cols) == (iota(wide, 1) + epoch * part) // (cols // mask_cols)
    to_cols = ones_where(to_cols)

    def depth_from(groups):
        messages = [message[e] for message in groups for e in range(epochs)]
        every = jnp.concatenate([m[:held_slots].astype(F32) for m in messages], 0)
        prior_total = jnp.zeros((8, 1), F32)
        for message in messages[::epochs]:
            message = message[held_slots : held_slots + 8].astype(F32)
            prior_total = prior_total + jnp.sum(message[:, PRIOR_LANE : PRIOR_LANE + 3], 1, keepdims=True)
        number = every.shape[0]
        taps = slot_taps(every)
        cover = cover_ref.at[:number]
        cover[...] = column_cover(every, taps, 0, cols)
        at = iota((number, LANES), 1)

        def row_cover(row):
            total = jnp.zeros(row.shape, F32)
            for t in range(TAPS):
                total = total + jnp.where(between(row + float(t - REACH), rows), taps[:, 8 + t : 9 + t], 0.0)
            return jnp.clip(total, 0.0, 1.0)

        tile = column(every, TILE)
        row = (at - MARGIN).astype(F32)
        canvas_cover = row_cover(row - column(every, DY))
        in_patch = between(row + tile * float(rows), sky * rows) & (at < canvas)
        canvas_cover = jnp.where(in_patch, canvas_cover, 0.0)
        area = dot(canvas_cover.astype(BF16), by_block) * dot(cover[...].astype(BF16), by_cell)
        area = jnp.where(at < field_at, every * area, 0.0)
        area = jnp.sum(area, 1, keepdims=True)
        precision = [1.0 / (column(every, SIGMA + b) * column(every, SIGMA + b)) for b in range(bands)]
        totals = []
        for b in range(bands):
            total = jnp.sum(area * jnp.where(tile >= 0.0, precision[b], 0.0), 0, keepdims=True)
            totals.append(total + prior_total[b : b + 1] * float(cols))
        group_rows = rows // BLOCK_ROWS
        wide = (number, bands * rows)
        in_band = iota(wide, 1)
        row = (lax.rem(in_band, rows) + me * rows).astype(F32) - tile * float(rows) - column(every, DY)
        profile = row_cover(row)
        factor = jnp.zeros(wide, F32)
        for b in range(bands):
            factor = jnp.where(in_band // rows == b, precision[b], factor)
        profile = profile * factor
        block = lax.rem(in_band, rows) // BLOCK_ROWS
        lhs = jnp.concatenate([jnp.where(block == g, profile, 0.0) for g in range(group_rows)], 0).astype(BF16)
        first = MARGIN // BLOCK_ROWS
        canvas_block = (first + group_rows * me).astype(F32) - tile * float(group_rows)
        chosen = [
            jnp.where(((at // mask_cols).astype(F32) == canvas_block + float(g)) & (at < field_at), every, 0.0)
            for g in range(group_rows)
        ]
        cells = dot(jnp.concatenate(chosen, 0).astype(BF16), to_cols)
        own_cover = cover[:, own_cols]
        cells = (cells * jnp.concatenate([own_cover] * group_rows, 0)).astype(BF16)
        return (dot_first(lhs, cells), *totals)

    if sky <= AT_ONCE:
        weights, *totals = depth_from([group[...]] + [others[d - 1] for d in range(1, sky)])
    else:
        weights, *totals = lax.fori_loop(
            0, sky - 1,
            lambda d, sums: tuple(x + y for x, y in zip(sums, depth_from([others[d]]))),
            depth_from([group[...]]),
        )
    means = [total * (1.0 / (sky * rows * cols)) for total in totals]
    diagonal = iota((rows, rows), 0) == iota((rows, rows), 1)
    depths = []
    for b in range(bands):
        prior = jnp.sum(jnp.where(diagonal, prior_ref[b : b + 1], 0.0), 1, keepdims=True)
        depth = weights[b * rows : (b + 1) * rows] + prior
        depth_ref[b] = (depth / means[b]).astype(BF16)
        depths.append(depth)
    for b in range(bands):
        total = flux[b, own_rows]
        for d in range(1, sky):
            flux_copies[d, b].wait_recv()
            total = total + held[d - 1, b].astype(F32)
        coadd_ref[b] = (framed[b, own_rows] + total / depths[b]).astype(BF16)
    for copies in (group_copies, others_copies, template_copies, columns_copies, flux_copies):
        for copy in copies.values():
            copy.wait_send()


def on_device(
    slot_pixels, slot_tile, slot_offset, slot_frac, slot_sigma, clip_mask, slot_count, template, prior_weight
):
    sky = lax.axis_size("sky")
    epochs = lax.axis_size("epoch")
    slots, bands, rows, cols = slot_pixels.shape
    blocks, mask_cols = clip_mask.shape[1:]
    part = cols // epochs
    canvas = rows + 2 * MARGIN
    held_slots = slots + -slots % 8
    field_rows = SIGMA + bands + -(SIGMA + bands) % 8
    message = held_slots + field_rows
    at_once = sky if sky <= AT_ONCE else 1
    pairs = at_once * CAPACITY
    vmem = pl.BlockSpec(memory_space=pltpu.VMEM)
    smem = pl.BlockSpec(memory_space=pltpu.SMEM)
    block = jax.ShapeDtypeStruct((bands, rows, part), BF16)
    patch = sky * rows + 2 * MARGIN
    return pl.pallas_call(
        functools.partial(coadd_kernel, (bands, sky, epochs, rows, cols, slots, blocks, mask_cols)),
        out_shape=(block, block),
        in_specs=[smem] * 2 + [vmem] * 7 + [pl.BlockSpec(memory_space=pl.ANY)],
        out_specs=(vmem, vmem),
        scratch_shapes=[
            pltpu.VMEM((bands, slots, rows, cols), BF16),
            pltpu.VMEM((field_rows, LANES), F32),
            pltpu.VMEM((epochs, message, LANES), BF16),
            pltpu.VMEM((sky - 1, epochs, message, LANES), BF16),
            pltpu.VMEM((TAPS, held_slots, LANES), F32),
            pltpu.VMEM((epochs, bands, slots * rows, part), BF16),
            pltpu.VMEM((epochs - 1, bands, slots * rows, part), BF16),
            pltpu.VMEM((sky - 1, bands, rows, part), BF16),
            pltpu.VMEM((bands, patch, part), F32),
            pltpu.VMEM((bands, patch, part), F32),
            pltpu.VMEM((epochs, pairs * canvas, slots * rows), BF16),
            pltpu.VMEM((epochs, bands, pairs * canvas, part), F32),
            pltpu.VMEM((epochs, bands, pairs, LANES), F32),
            pltpu.VMEM((pairs * canvas, part), F32),
            pltpu.VMEM((sky - 1, bands, rows, part), BF16),
            pltpu.VMEM((sky - 1, bands, rows, part), BF16),
            pltpu.VMEM(((sky if sky <= AT_ONCE else 1) * epochs * held_slots, cols), F32),
            pltpu.SemaphoreType.DMA((bands,)),
            pltpu.SemaphoreType.DMA((2, epochs - 1)),
            pltpu.SemaphoreType.DMA((2, sky - 1)),
            pltpu.SemaphoreType.DMA((2, sky - 1, bands)),
            pltpu.SemaphoreType.DMA((2, epochs - 1, bands)),
            pltpu.SemaphoreType.DMA((2, sky - 1, bands)),
        ],
        compiler_params=pltpu.CompilerParams(collective_id=0, has_side_effects=True),
        name="coadd",
    )(
        slot_offset.T, slot_count, slot_tile.T, slot_offset.T, slot_frac.T, slot_sigma.T, clip_mask,
        template, prior_weight, slot_pixels,
    )


def solution(mesh):
    in_specs = (
        P(("groups", "sky", "epoch"), "band", None, None),
        P(("groups", "sky", "epoch"), None),
        P(("groups", "sky", "epoch"), None),
        P(("groups", "sky", "epoch"), None),
        P(("groups", "sky", "epoch"), "band"),
        P(("groups", "sky", "epoch"), None, None),
        P(("groups", "sky", "epoch")),
        P("band", ("groups", "sky"), None),
        P("band", ("groups", "sky")),
    )
    out_specs = (P("band", ("groups", "sky"), "epoch"), P("band", ("groups", "sky"), "epoch"))
    return jax.shard_map(
        on_device, mesh=mesh, in_specs=in_specs, out_specs=out_specs, check_vma=False
    )
```

time: 45 us -> 23.1 us (0.51)
  Pallas kernels: 38.8 us -> 19.5 us
  local copies, waits for them, and re-layouts: 4.35 us -> 2.06 us
    pallas_call x3 -> x1, Pallas kernels: 38.8 us -> 19.5 us  [on_device(): pl.pallas_call(functools.partial(coadd_kernel, (bands, sky, epochs, rows,...]
    unnamed x9 -> x4, local copies, waits for them, and re-layouts: 3.48 us -> 2.06 us
    concatenate x1 -> x0, local copies, waits for them, and re-layouts: 0.71 us -> none  [on_device(): jnp.concatenate([taps, scale, 1.0 / scale, 1.0 / (sigma * sigma)], 0)]
where the time goes in v1:
time: 23.1 us; the launch traced here: 22.9 us
  Pallas kernels  19.5 us (84%)
  local copies, waits for them, and re-layouts  2.06 us (9%)
  between operations  1.3 us (6%)
    pallas_call x1, Pallas kernels, on_device(): pl.pallas_call(functools.partial(coadd_kernel, (bands, sky, epochs, rows,...  19.5 us
    unnamed x4, local copies, waits for them, and re-layouts  2.06 us

profile of v1, /device:TPU:0, one launch (start us, length us, event | category | flops | bytes accessed | tf_op | source)
XLA Modules:
  0.0 22.9 jit_solution(9002645993647142283)
XLA Ops:
  1.3 19.5 %coadd.1 = (bf16[3,32,256]{2,1,0:T(8,128)(2,1)}, bf16[3,32,256]{2,1,0:T(8,128)(2,1)}) custom-call(s32[2,6]{1,0:T(2,128)} %bitcast.4, s32[1]{0:T(128)S(6)} %copy.13.count_ref, s32[1,6]{1,0:T(1,128)} %bitcast.7, s32[2,6]{1,0:T(2,128)} %bitcast.5, bf16[2,6]{1,0:T(2,128)(2,1)} %bitcast.8, bf16[3,6]{1,0:T(4,128)(2,1)} %bitcast.6, s32[6,6,16]{2,1,0:T(8,128)} %mask_ref.1, ...), custom_call_target="tpu_custom_call" | custom-call | tf_op jit(solution)/shard_map/coadd/pallas_call | solution.py:439
  20.8 0.0 copy-start
  20.8 1.4 %copy.14 = bf16[3,32,256]{2,1,0:T(8,128)(2,1)} copy(bf16[3,32,256]{2,1,0:T(8,128)(2,1)} %get-tuple-element.4) | data formatting | bytes 98304
  22.3 0.0 copy-done
  22.3 0.6 %copy.15 = bf16[3,32,256]{2,1,0:T(8,128)(2,1)} copy(bf16[3,32,256]{2,1,0:T(8,128)(2,1)S(1)} %copy-done) | data formatting | bytes 98304
Async XLA Ops:
  20.8 1.4 %copy-start = (bf16[3,32,256]{2,1,0:T(8,128)(2,1)S(1)}, bf16[3,32,256]{2,1,0:T(8,128)(2,1)}, u32[]{:S(2)}) copy-start(bf16[3,32,256]{2,1,0:T(8,128)(2,1)} %get-tuple-element.5) | copy-start | bytes 147460

commit v2 on v1

--- a/solution.py
+++ b/solution.py
@@ -60,13 +60,16 @@
 
 
 def coadd_kernel(
-    shape, steer_ref, count_ref, tile_ref, offset_ref, frac_ref, sigma_ref, mask_ref,
-    template_ref, prior_ref, pixels_ref,
-    coadd_ref, depth_ref,
-    pixels, small, group, others, tap_table, columns, columns_held, template_held,
-    framed, flux, left, weigh, inverse, warped, send, held, cover_ref,
-    local_sem, group_sem, others_sem, template_sem, columns_sem, flux_sem,
+    shape, *refs,
 ):
+    count_ref, *inputs = refs[:9]
+    (
+        coadd_ref, depth_ref,
+        offset_ref, frac_ref, template_ref, tile_ref, sigma_ref, mask_ref, prior_ref,
+        pixels, small, group, others, tap_table, lag_ref, kernel_x, columns, columns_held, template_held,
+        framed, flux, left, weigh, inverse, warped, send, held, cover_ref,
+        local_sem, group_sem, others_sem, template_sem, columns_sem, flux_sem,
+    ) = refs[9:]
     bands, sky, epochs, rows, cols, slots, blocks, mask_cols = shape
     part = cols // epochs
     canvas = rows + 2 * MARGIN
@@ -91,11 +94,15 @@
         pl.semaphore_signal(barrier, inc=1, device_id={"sky": sky_peer(d)}, device_id_type=MESH)
     for d in range(1, epochs):
         pl.semaphore_signal(barrier, inc=1, device_id={"epoch": epoch_peer(d)}, device_id_type=MESH)
+    targets = [offset_ref, frac_ref] + [pixels.at[b] for b in range(bands)] + [
+        template_ref, tile_ref, sigma_ref, mask_ref, prior_ref
+    ]
+    sources = inputs[:2] + [inputs[2].at[:, b] for b in range(bands)] + inputs[3:]
     loads = []
-    for b in range(bands):
-        load = pltpu.make_async_copy(pixels_ref.at[:, b], pixels.at[b], local_sem.at[b])
-        load.start()
-        loads.append(load)
+    for i, (source, target) in enumerate(zip(sources, targets)):
+        loads.append(pltpu.make_async_copy(source, target, local_sem.at[i]))
+        loads[-1].start()
+    pixel_loads, loads = loads[2 : 2 + bands], loads[:2] + loads[2 + bands :]
 
     def remote(src, dst, sems, index, where):
         copy = pltpu.make_async_remote_copy(
@@ -105,6 +112,60 @@
         copy.start()
         return copy
 
+    tall = (2 * LANES, LANES)
+    reached = LANES + 2 * MARGIN
+    source_at = jnp.where(iota(tall, 0) < 3 * LANES // 2, iota(tall, 0), iota(tall, 0) - 2 * LANES)
+    lag_ref[...] = (source_at - iota(tall, 1)).astype(F32)
+    idle = jnp.zeros((2 * LANES - 2 * MARGIN - reached, LANES), BF16)
+    for p in range(slots):
+        kernel_x[p, reached : 2 * LANES - 2 * MARGIN] = idle
+    for load in loads[:2]:
+        load.wait()
+    tap_rows = jnp.broadcast_to(frac_ref[1:2].astype(F32), (8, slots))
+    tap_rows = rounded(lanczos((REACH - iota((8, slots), 0)).astype(F32) - tap_rows))
+    lag_rows = (iota((8, slots), 0) - REACH - jnp.broadcast_to(offset_ref[1:2], (8, slots))).astype(F32)
+    for p in range(slots):
+        tap_table[0, p] = jnp.broadcast_to(tap_rows[:, p : p + 1], (8, LANES))
+        tap_table[1, p] = jnp.broadcast_to(lag_rows[:, p : p + 1], (8, LANES))
+    ahead = ones_where(iota((rows, LANES), 1) < LANES // 2)
+    behind = ones_where(iota((rows, LANES), 1) >= LANES // 2)
+
+    def over_slots(step):
+        lax.fori_loop(0, slots, lambda p, c: (step(p), c)[1], 0, unroll=slots <= 8)
+
+    def build_kernel(p):
+        for part_rows in (slice(0, reached), slice(2 * LANES - 2 * MARGIN, 2 * LANES)):
+            lag = lag_ref[part_rows]
+            total = jnp.zeros(lag.shape, F32)
+            for t in range(TAPS):
+                total = jnp.where(lag == tap_table[1, p, t : t + 1], tap_table[0, p, t : t + 1], total)
+            kernel_x[p, part_rows] = total.astype(BF16)
+
+    def warp_columns(b):
+        def one_slot(p):
+            count = cols // LANES
+            source = [pixels[b, p, :, c * LANES : (c + 1) * LANES] for c in range(count)]
+            blocks_in = []
+            for c in range(count):
+                beside = jnp.zeros((rows, LANES), BF16)
+                if c + 1 < count:
+                    beside = source[c + 1] * ahead
+                if c:
+                    beside = beside + source[c - 1] * behind
+                blocks_in.append(jnp.concatenate([source[c], beside], 1))
+            summed = dot(jnp.concatenate(blocks_in, 0), kernel_x[p]).astype(BF16)
+            here = pl.ds(pl.multiple_of(p * rows, rows), rows)
+            for c in range(count):
+                e, first = c * LANES // part, c * LANES % part
+                columns[e, b, here, first : first + LANES] = summed[c * rows : (c + 1) * rows]
+
+        over_slots(one_slot)
+
+    pixel_loads[0].wait()
+    for load in loads[2:]:
+        load.wait()
+    over_slots(build_kernel)
+    warp_columns(0)
     lane = iota((8, LANES), 1)
     small[...] = jnp.ones_like(small)
     tile = jnp.where(iota((1, slots), 1) < count_ref[0], tile_ref[...].astype(F32), NOBODY)
@@ -158,51 +219,24 @@
             total = total + jnp.where(between(at + float(t - REACH), cols), taps[:, t : t + 1], 0.0)
         return jnp.clip(total, 0.0, 1.0)
 
-    taps = slot_taps(by_slot)
-    for t in range(TAPS):
-        tap_table[t] = jnp.broadcast_to(taps[:, t : t + 1], (held_slots, LANES))
-
-    def warp_columns(b):
-        def one_slot(p, carry):
-            source = jnp.concatenate([pixels[b, p].astype(F32), jnp.zeros((rows, LANES), F32)], 1)
-            base = pltpu.roll(source, lax.rem(steer_ref[1, p] + padded, padded), 1)
-
-            def tap(t):
-                return jnp.concatenate([tap_table[t, pl.ds(p, 1)]] * (padded // LANES), 1)
-
-            summed = tap(REACH) * base
-            for t in range(TAPS):
-                if t != REACH:
-                    summed = summed + tap(t) * pltpu.roll(base, (REACH - t) % padded, 1)
-            at = pl.ds(pl.multiple_of(p * rows, rows), rows)
-            for e in range(epochs):
-                columns[e, b, at] = summed[:, e * part : (e + 1) * part].astype(BF16)
-            return carry
-
-        lax.fori_loop(0, slots, one_slot, 0, unroll=slots <= 8)
-
-    started = []
     columns_copies, template_copies, group_copies, others_copies, flux_copies = {}, {}, {}, {}, {}
+    pl.semaphore_wait(barrier, sky - 1 + epochs - 1)
+    for d in range(1, epochs):
+        group_copies[d] = remote(group.at[0], group.at[d], group_sem, (d - 1,), {"epoch": epoch_peer(d)})
     for b in range(bands):
-        loads[b].wait()
-        warp_columns(b)
-        if b == 0:
-            pl.semaphore_wait(barrier, sky - 1 + epochs - 1)
-            for d in range(1, epochs):
-                group_copies[d] = remote(
-                    group.at[0], group.at[d], group_sem, (d - 1,), {"epoch": epoch_peer(d)}
-                )
+        if b:
+            pixel_loads[b].wait()
+            warp_columns(b)
+        for d in range(1, epochs):
+            columns_copies[d, b] = remote(
+                columns.at[epoch_peer(d), b], columns_held.at[d - 1, b], columns_sem, (d - 1, b),
+                {"epoch": epoch_peer(d)},
+            )
         for d in range(1, sky):
             template_copies[d, b] = remote(
                 template_ref.at[b, :, own_cols], template_held.at[d - 1, b], template_sem, (d - 1, b),
                 {"sky": sky_peer(d)},
             )
-        for d in range(1, epochs):
-            columns_copies[d, b] = remote(
-                columns.at[epoch_peer(d), b], columns_held.at[d - 1, b], columns_sem, (d - 1, b),
-                {"epoch": epoch_peer(d)},
-            )
-
     flux[...] = jnp.zeros_like(flux)
     edge = jnp.zeros((bands, MARGIN, part), F32)
     framed[:, :MARGIN] = edge
@@ -418,6 +452,17 @@
             copy.wait_send()
 
 
+def leave_kernel(coadd_in, depth_in, coadd_ref, depth_ref, sem):
+    copies = [
+        pltpu.make_async_copy(coadd_in, coadd_ref, sem.at[0]),
+        pltpu.make_async_copy(depth_in, depth_ref, sem.at[1]),
+    ]
+    for copy in copies:
+        copy.start()
+    for copy in copies:
+        copy.wait()
+
+
 def on_device(
     slot_pixels, slot_tile, slot_offset, slot_frac, slot_sigma, clip_mask, slot_count, template, prior_weight
 ):
@@ -433,20 +478,29 @@
     at_once = sky if sky <= AT_ONCE else 1
     pairs = at_once * CAPACITY
     vmem = pl.BlockSpec(memory_space=pltpu.VMEM)
-    smem = pl.BlockSpec(memory_space=pltpu.SMEM)
     block = jax.ShapeDtypeStruct((bands, rows, part), BF16)
     patch = sky * rows + 2 * MARGIN
-    return pl.pallas_call(
+    limit = 32 * 1024 * 1024 if sky <= AT_ONCE else None
+    results = pl.pallas_call(
         functools.partial(coadd_kernel, (bands, sky, epochs, rows, cols, slots, blocks, mask_cols)),
         out_shape=(block, block),
-        in_specs=[smem] * 2 + [vmem] * 7 + [pl.BlockSpec(memory_space=pl.ANY)],
+        in_specs=[pl.BlockSpec(memory_space=pltpu.SMEM)] + [pl.BlockSpec(memory_space=pltpu.MemorySpace.HBM)] * 8,
         out_specs=(vmem, vmem),
         scratch_shapes=[
+            pltpu.VMEM((2, slots), jnp.int32),
+            pltpu.VMEM((2, slots), BF16),
+            pltpu.VMEM((bands, rows, cols), BF16),
+            pltpu.VMEM((1, slots), jnp.int32),
+            pltpu.VMEM((bands, slots), BF16),
+            pltpu.VMEM((slots, blocks, mask_cols), jnp.int32),
+            pltpu.VMEM((bands, rows), F32),
             pltpu.VMEM((bands, slots, rows, cols), BF16),
             pltpu.VMEM((field_rows, LANES), F32),
             pltpu.VMEM((epochs, message, LANES), BF16),
             pltpu.VMEM((sky - 1, epochs, message, LANES), BF16),
-            pltpu.VMEM((TAPS, held_slots, LANES), F32),
+            pltpu.VMEM((2, slots, 8, LANES), F32),
+            pltpu.VMEM((2 * LANES, LANES), F32),
+            pltpu.VMEM((slots, 2 * LANES, LANES), BF16),
             pltpu.VMEM((epochs, bands, slots * rows, part), BF16),
             pltpu.VMEM((epochs - 1, bands, slots * rows, part), BF16),
             pltpu.VMEM((sky - 1, bands, rows, part), BF16),
@@ -459,19 +513,32 @@
             pltpu.VMEM((sky - 1, bands, rows, part), BF16),
             pltpu.VMEM((sky - 1, bands, rows, part), BF16),
             pltpu.VMEM(((sky if sky <= AT_ONCE else 1) * epochs * held_slots, cols), F32),
-            pltpu.SemaphoreType.DMA((bands,)),
+            pltpu.SemaphoreType.DMA((bands + 7,)),
             pltpu.SemaphoreType.DMA((2, epochs - 1)),
             pltpu.SemaphoreType.DMA((2, sky - 1)),
             pltpu.SemaphoreType.DMA((2, sky - 1, bands)),
             pltpu.SemaphoreType.DMA((2, epochs - 1, bands)),
             pltpu.SemaphoreType.DMA((2, sky - 1, bands)),
         ],
-        compiler_params=pltpu.CompilerParams(collective_id=0, has_side_effects=True),
+        compiler_params=pltpu.CompilerParams(collective_id=0, has_side_effects=True, vmem_limit_bytes=limit),
         name="coadd",
-    )(
-        slot_offset.T, slot_count, slot_tile.T, slot_offset.T, slot_frac.T, slot_sigma.T, clip_mask,
-        template, prior_weight, slot_pixels,
-    )
+    )(*[
+        x if x is slot_count else pltpu.with_memory_space_constraint(x, pltpu.MemorySpace.HBM)
+        for x in (
+            slot_count, slot_offset.T, slot_frac.T, slot_pixels, template, slot_tile.T, slot_sigma.T,
+            clip_mask, prior_weight,
+        )
+    ])
+
+    return pl.pallas_call(
+        leave_kernel,
+        out_shape=(block, block),
+        in_specs=[vmem] * 2,
+        out_specs=(pl.BlockSpec(memory_space=pl.ANY),) * 2,
+        scratch_shapes=[pltpu.SemaphoreType.DMA((2,))],
+        compiler_params=pltpu.CompilerParams(vmem_limit_bytes=1024 * 1024),
+        name="leave",
+    )(*results)
 
 
 def solution(mesh):

time: 23.1 us -> 20.2 us (0.87)
  local copies, waits for them, and re-layouts: 2.06 us -> 0 us
  Pallas kernels: 19.5 us -> 18.7 us
    unnamed x4 -> x0, local copies, waits for them, and re-layouts: 2.06 us -> none
    pallas_call x1, Pallas kernels: 19.5 us -> 18 us  [on_device(): pl.pallas_call(functools.partial(coadd_kernel, (bands, sky, epochs, rows,...]
    pallas_call x0 -> x1, Pallas kernels: none -> 0.66 us  [on_device(): pl.pallas_call(leave_kernel, out_shape=(block, block), in_specs=[vmem] *...]
where the time goes in v2:
time: 20.2 us; the launch traced here: 20 us
  Pallas kernels  18.7 us (93%)
  between operations  1.29 us (6%)
    pallas_call x1, Pallas kernels, on_device(): pl.pallas_call(functools.partial(coadd_kernel, (bands, sky, epochs, rows,...  18 us
    pallas_call x1, Pallas kernels, on_device(): pl.pallas_call(leave_kernel, out_shape=(block, block), in_specs=[vmem] *...  0.66 us

profile of v2, /device:TPU:0, one launch (start us, length us, event | category | flops | bytes accessed | tf_op | source)
XLA Modules:
  0.0 20.0 jit_solution(3525245476775272190)
XLA Ops:
  1.3 18.0 %coadd.1 = (bf16[3,32,256]{2,1,0:T(8,128)(2,1)S(1)}, bf16[3,32,256]{2,1,0:T(8,128)(2,1)S(1)}) custom-call(s32[1]{0:T(128)S(6)} %copy.11.refs_0_, s32[2,6]{1,0:T(2,128)} %bitcast.4, bf16[2,6]{1,0:T(2,128)(2,1)} %bitcast.6, bf16[6,3,32,512]{3,2,1,0:T(8,128)(2,1)} %refs_3_.1, bf16[3,32,512]{2,1,0:T(8,128)(2,1)} %refs_4_.1, s32[1,6]{1,0:T(1,128)} %bitcast.7, ...), custom_call_target="tpu_custom_call" | custom-call | tf_op jit(solution)/shard_map/coadd/pallas_call | solution.py:484
  19.3 0.7 %leave.1 = (bf16[3,32,256]{2,1,0:T(8,128)(2,1)}, bf16[3,32,256]{2,1,0:T(8,128)(2,1)}) custom-call(bf16[3,32,256]{2,1,0:T(8,128)(2,1)S(1)} %get-tuple-element.4.coadd_in, bf16[3,32,256]{2,1,0:T(8,128)(2,1)S(1)} %get-tuple-element.5.depth_in), custom_call_target="tpu_custom_call" | custom-call | tf_op jit(solution)/shard_map/leave/pallas_call | solution.py:533

commit v3 on v2

--- a/solution.py
+++ b/solution.py
@@ -23,41 +23,32 @@
 F32 = jnp.float32
 BF16 = jnp.bfloat16
 
-
 def sinc(x):
     at_zero = x == 0.0
     turned = math.pi * jnp.where(at_zero, 1.0, x)
     return jnp.where(at_zero, 1.0, jnp.sin(turned) / turned)
 
-
 def lanczos(distance):
     inside = jnp.abs(distance) < 3.0
     return jnp.where(inside, sinc(distance) * sinc(distance / 3.0), 0.0)
 
-
 def rounded(x):
     return x.astype(BF16).astype(F32)
 
-
 def iota(shape, dim):
     return lax.broadcasted_iota(jnp.int32, shape, dim)
 
-
 def ones_where(condition):
     return jnp.where(condition, 1.0, 0.0).astype(BF16)
 
-
 def dot(a, b):
     return jnp.dot(a, b, preferred_element_type=F32)
 
-
 def dot_first(a, b):
     return lax.dot_general(a, b, (((0,), (0,)), ((), ())), preferred_element_type=F32)
 
-
 def between(x, extent):
     return (x >= 0.0) & (x < float(extent))
-
 
 def coadd_kernel(
     shape, *refs,
@@ -67,8 +58,8 @@
         coadd_ref, depth_ref,
         offset_ref, frac_ref, template_ref, tile_ref, sigma_ref, mask_ref, prior_ref,
         pixels, small, group, others, tap_table, lag_ref, kernel_x, columns, columns_held, template_held,
-        framed, flux, left, weigh, inverse, warped, send, held, cover_ref,
-        local_sem, group_sem, others_sem, template_sem, columns_sem, flux_sem,
+        framed, flux, left, weigh, inverse, send, held, cover_ref,
+        local_sem, message_sem, template_sem, columns_sem, flux_sem, sent_sem,
     ) = refs[9:]
     bands, sky, epochs, rows, cols, slots, blocks, mask_cols = shape
     part = cols // epochs
@@ -94,23 +85,27 @@
         pl.semaphore_signal(barrier, inc=1, device_id={"sky": sky_peer(d)}, device_id_type=MESH)
     for d in range(1, epochs):
         pl.semaphore_signal(barrier, inc=1, device_id={"epoch": epoch_peer(d)}, device_id_type=MESH)
-    targets = [offset_ref, frac_ref] + [pixels.at[b] for b in range(bands)] + [
-        template_ref, tile_ref, sigma_ref, mask_ref, prior_ref
-    ]
-    sources = inputs[:2] + [inputs[2].at[:, b] for b in range(bands)] + inputs[3:]
+    targets = [offset_ref, frac_ref, pixels.at[0], template_ref, tile_ref, sigma_ref, mask_ref, prior_ref]
+    targets += [pixels.at[b] for b in range(1, bands)]
+    sources = inputs[:2] + [inputs[2].at[:, 0]] + inputs[3:] + [inputs[2].at[:, b] for b in range(1, bands)]
     loads = []
     for i, (source, target) in enumerate(zip(sources, targets)):
         loads.append(pltpu.make_async_copy(source, target, local_sem.at[i]))
         loads[-1].start()
-    pixel_loads, loads = loads[2 : 2 + bands], loads[:2] + loads[2 + bands :]
-
-    def remote(src, dst, sems, index, where):
-        copy = pltpu.make_async_remote_copy(
-            src_ref=src, dst_ref=dst, send_sem=sems.at[(0,) + index], recv_sem=sems.at[(1,) + index],
-            device_id=where, device_id_type=MESH,
-        )
-        copy.start()
-        return copy
+
+    def remote(src, dst, sent, received, where):
+        pltpu.make_async_remote_copy(
+            src_ref=src, dst_ref=dst, send_sem=sent, recv_sem=received, device_id=where, device_id_type=MESH
+        ).start()
+
+    def wait_bytes(ref, sem):
+        pltpu.make_async_copy(ref, ref, sem).wait()
+
+    halves = 2 if part % (2 * LANES) == 0 else 1
+    chunks = []
+    for b in range(bands):
+        pieces = halves if b in (0, bands - 1) else 1
+        chunks += [(b, i * (part // pieces), part // pieces) for i in range(pieces)]
 
     tall = (2 * LANES, LANES)
     reached = LANES + 2 * MARGIN
@@ -161,9 +156,33 @@
 
         over_slots(one_slot)
 
-    pixel_loads[0].wait()
-    for load in loads[2:]:
+    near_core = lax.axis_index("band") > 0
+
+    def send_columns(i):
+        if chunks[i][0] == 0:
+            send_columns_now(i)
+        else:
+            pl.when(jnp.logical_not(near_core))(functools.partial(send_columns_now, i))
+
+    def send_columns_now(i):
+        b, first, width = chunks[i]
+        at = pl.ds(first, width)
+        for d in range(1, epochs):
+            remote(
+                columns.at[epoch_peer(d), b, :, at], columns_held.at[d - 1, b, :, at],
+                sent_sem.at[0], columns_sem.at[i], {"epoch": epoch_peer(d)},
+            )
+
+    def send_template(b):
+        for d in range(1, sky):
+            remote(
+                template_ref.at[b, :, own_cols], template_held.at[d - 1, b],
+                sent_sem.at[1], template_sem.at[b], {"sky": sky_peer(d)},
+            )
+
+    for load in loads[2:8]:
         load.wait()
+
     over_slots(build_kernel)
     warp_columns(0)
     lane = iota((8, LANES), 1)
@@ -219,24 +238,23 @@
             total = total + jnp.where(between(at + float(t - REACH), cols), taps[:, t : t + 1], 0.0)
         return jnp.clip(total, 0.0, 1.0)
 
-    columns_copies, template_copies, group_copies, others_copies, flux_copies = {}, {}, {}, {}, {}
     pl.semaphore_wait(barrier, sky - 1 + epochs - 1)
+
     for d in range(1, epochs):
-        group_copies[d] = remote(group.at[0], group.at[d], group_sem, (d - 1,), {"epoch": epoch_peer(d)})
-    for b in range(bands):
-        if b:
-            pixel_loads[b].wait()
-            warp_columns(b)
-        for d in range(1, epochs):
-            columns_copies[d, b] = remote(
-                columns.at[epoch_peer(d), b], columns_held.at[d - 1, b], columns_sem, (d - 1, b),
-                {"epoch": epoch_peer(d)},
-            )
-        for d in range(1, sky):
-            template_copies[d, b] = remote(
-                template_ref.at[b, :, own_cols], template_held.at[d - 1, b], template_sem, (d - 1, b),
-                {"sky": sky_peer(d)},
-            )
+        remote(group.at[0], group.at[d], sent_sem.at[2], message_sem.at[0], {"epoch": epoch_peer(d)})
+    for i in range(halves):
+        send_columns(i)
+    send_template(0)
+    for b in range(1, bands):
+
+        loads[7 + b].wait()
+        warp_columns(b)
+
+        for i, chunk in enumerate(chunks):
+            if chunk[0] == b:
+                send_columns(i)
+        send_template(b)
+
     flux[...] = jnp.zeros_like(flux)
     edge = jnp.zeros((bands, MARGIN, part), F32)
     framed[:, :MARGIN] = edge
@@ -311,19 +329,22 @@
         for b in range(bands):
             weigh[d, b] = dot(jnp.concatenate(lhs[b], 0).astype(BF16), cells)
 
-    def process(d, b, first_owner):
-        source = columns[epoch, b] if d == 0 else columns_held[d - 1, b]
-        warped[...] = dot(left[d], source)
+    def process(d, chunk, first_owner):
+        b, first, width = chunk
+        lanes = slice(first, first + width)
+        source = columns[epoch, b, :, lanes] if d == 0 else columns_held[d - 1, b, :, lanes]
         for o in range(at_once):
             at = pl.ds(pl.multiple_of((first_owner + o) * rows, 8), canvas)
-            frame = framed[b, at]
-            total = flux[b, at]
+            frame = framed[b, at, lanes]
+            total = flux[b, at, lanes]
+            both = slice(o * CAPACITY * canvas, (o + 1) * CAPACITY * canvas)
+            warped = dot(left[d, both], source)
             for k in range(CAPACITY):
                 pair = o * CAPACITY + k
                 here = slice(pair * canvas, (pair + 1) * canvas)
-                scale = jnp.concatenate([inverse[d, b, pair : pair + 1]] * (part // LANES), 1)
-                total = total + weigh[d, b, here] * jnp.tanh((warped[here] - frame) * scale)
-            flux[b, at] = total
+                scale = jnp.concatenate([inverse[d, b, pair : pair + 1]] * (width // LANES), 1)
+                total = total + weigh[d, b, here, lanes] * jnp.tanh((warped[k * canvas : (k + 1) * canvas] - frame) * scale)
+            flux[b, at, lanes] = total
 
     def all_owners(step):
         if sky == at_once:
@@ -331,37 +352,60 @@
         else:
             lax.fori_loop(0, sky // at_once, lambda i, c: (step(i * at_once), c)[1], 0)
 
-    for d in range(1, epochs):
-        group_copies[d].wait_recv()
-    for d in range(1, sky):
-        others_copies[d] = remote(group, others.at[d - 1], others_sem, (d - 1,), {"sky": sky_peer(d)})
     if sky == at_once:
+        prepare(0, 0)
+
+    def send_held_back():
+        for i, chunk in enumerate(chunks):
+            if chunk[0] > 0:
+                send_columns_now(i)
+
+    def meet_epoch_peers():
+        wait_bytes(group.at[1:], message_sem.at[0])
+        for d in range(1, sky):
+            remote(group, others.at[d - 1], sent_sem.at[3], message_sem.at[1], {"sky": sky_peer(d)})
+        if sky == at_once:
+
+            for d in range(1, epochs):
+                prepare(d, 0)
+
+    meet_epoch_peers()
+    for i, chunk in enumerate(chunks):
+        b, first, width = chunk
+        lanes = slice(first, first + width)
+        if first == 0:
+
+            wait_bytes(template_held.at[:, b], template_sem.at[b])
+            for d in range(1, sky):
+                at = pl.ds(pl.multiple_of(MARGIN + lax.rem(me - d + sky, sky) * rows, 8), rows)
+                framed[b, at] = template_held[d - 1, b].astype(F32)
+        if i == 0:
+            pl.when(near_core)(send_held_back)
         for d in range(epochs):
-            prepare(d, 0)
-    for b in range(bands):
-        for d in range(1, sky):
-            template_copies[d, b].wait_recv()
-            at = pl.ds(pl.multiple_of(MARGIN + lax.rem(me - d + sky, sky) * rows, 8), rows)
-            framed[b, at] = template_held[d - 1, b].astype(F32)
-        for d in range(epochs):
-            if d:
-                columns_copies[d, b].wait_recv()
-
-            def step(first_owner, d=d, b=b):
+            if d == 1:
+
+                wait_bytes(columns_held.at[:, b, :, pl.ds(first, width)], columns_sem.at[i])
+
+            def step(first_owner, d=d, chunk=chunk):
                 if sky != at_once:
                     prepare(d, first_owner)
-                process(d, b, first_owner)
+                process(d, chunk, first_owner)
 
             all_owners(step)
+
         for d in range(1, sky):
             at = pl.ds(pl.multiple_of(MARGIN + sky_peer(d) * rows, 8), rows)
-            send[d - 1, b] = flux[b, at].astype(BF16)
-            flux_copies[d, b] = remote(
-                send.at[d - 1, b], held.at[d - 1, b], flux_sem, (d - 1, b), {"sky": sky_peer(d)}
+            send[d - 1, b, :, lanes] = flux[b, at, lanes].astype(BF16)
+        for d in range(1, sky):
+            at = pl.ds(first, width)
+            remote(
+                send.at[d - 1, b, :, at], held.at[d - 1, b, :, at],
+                sent_sem.at[4], flux_sem.at[i], {"sky": sky_peer(d)},
             )
 
-    for d in range(1, sky):
-        others_copies[d].wait_recv()
+
+    wait_bytes(others, message_sem.at[1])
+
     square = (LANES, LANES)
     by_block = iota(square, 0) // BLOCK_ROWS == iota(square, 1) // mask_cols
     by_block = ones_where(by_block & (iota(square, 0) < canvas) & (iota(square, 1) < field_at))
@@ -441,16 +485,20 @@
         depth = weights[b * rows : (b + 1) * rows] + prior
         depth_ref[b] = (depth / means[b]).astype(BF16)
         depths.append(depth)
-    for b in range(bands):
-        total = flux[b, own_rows]
+
+    for sent, ref in enumerate((columns_held, template_held, group.at[1:], others)):
+        wait_bytes(ref, sent_sem.at[sent])
+    for i, (b, first, width) in enumerate(chunks):
+        lanes = slice(first, first + width)
+
+        wait_bytes(held.at[:, b, :, pl.ds(first, width)], flux_sem.at[i])
+
+        total = flux[b, own_rows, lanes]
         for d in range(1, sky):
-            flux_copies[d, b].wait_recv()
-            total = total + held[d - 1, b].astype(F32)
-        coadd_ref[b] = (framed[b, own_rows] + total / depths[b]).astype(BF16)
-    for copies in (group_copies, others_copies, template_copies, columns_copies, flux_copies):
-        for copy in copies.values():
-            copy.wait_send()
-
+            total = total + held[d - 1, b, :, lanes].astype(F32)
+        coadd_ref[b, :, lanes] = (framed[b, own_rows, lanes] + total / depths[b][:, lanes]).astype(BF16)
+
+    wait_bytes(send, sent_sem.at[4])
 
 def leave_kernel(coadd_in, depth_in, coadd_ref, depth_ref, sem):
     copies = [
@@ -461,7 +509,6 @@
         copy.start()
     for copy in copies:
         copy.wait()
-
 
 def on_device(
     slot_pixels, slot_tile, slot_offset, slot_frac, slot_sigma, clip_mask, slot_count, template, prior_weight
@@ -509,16 +556,15 @@
             pltpu.VMEM((epochs, pairs * canvas, slots * rows), BF16),
             pltpu.VMEM((epochs, bands, pairs * canvas, part), F32),
             pltpu.VMEM((epochs, bands, pairs, LANES), F32),
-            pltpu.VMEM((pairs * canvas, part), F32),
             pltpu.VMEM((sky - 1, bands, rows, part), BF16),
             pltpu.VMEM((sky - 1, bands, rows, part), BF16),
             pltpu.VMEM(((sky if sky <= AT_ONCE else 1) * epochs * held_slots, cols), F32),
             pltpu.SemaphoreType.DMA((bands + 7,)),
-            pltpu.SemaphoreType.DMA((2, epochs - 1)),
-            pltpu.SemaphoreType.DMA((2, sky - 1)),
-            pltpu.SemaphoreType.DMA((2, sky - 1, bands)),
-            pltpu.SemaphoreType.DMA((2, epochs - 1, bands)),
-            pltpu.SemaphoreType.DMA((2, sky - 1, bands)),
+            pltpu.SemaphoreType.DMA((2,)),
+            pltpu.SemaphoreType.DMA((bands,)),
+            pltpu.SemaphoreType.DMA((bands + 2,)),
+            pltpu.SemaphoreType.DMA((bands + 2,)),
+            pltpu.SemaphoreType.DMA((5,)),
         ],
         compiler_params=pltpu.CompilerParams(collective_id=0, has_side_effects=True, vmem_limit_bytes=limit),
         name="coadd",
@@ -539,7 +585,6 @@
         compiler_params=pltpu.CompilerParams(vmem_limit_bytes=1024 * 1024),
         name="leave",
     )(*results)
-
 
 def solution(mesh):
     in_specs = (

time: 20.2 us -> 19 us (0.941)
  Pallas kernels: 18.7 us -> 17.5 us
    pallas_call x1, Pallas kernels: 18 us -> 16.9 us  [on_device(): pl.pallas_call(functools.partial(coadd_kernel, (bands, sky, epochs, rows,...]
where the time goes in v3:
time: 19 us; the launch traced here: 18.8 us
  Pallas kernels  17.5 us (92%)
  between operations  1.29 us (7%)
    pallas_call x1, Pallas kernels, on_device(): pl.pallas_call(functools.partial(coadd_kernel, (bands, sky, epochs, rows,...  16.9 us
    pallas_call x1, Pallas kernels, on_device(): pl.pallas_call(leave_kernel, out_shape=(block, block), in_specs=[vmem] *...  0.66 us

profile of v3, /device:TPU:0, one launch (start us, length us, event | category | flops | bytes accessed | tf_op | source)
XLA Modules:
  0.0 18.8 jit_solution(293200580835275616)
XLA Ops:
  1.3 16.9 %coadd.1 = (bf16[3,32,256]{2,1,0:T(8,128)(2,1)S(1)}, bf16[3,32,256]{2,1,0:T(8,128)(2,1)S(1)}) custom-call(s32[1]{0:T(128)S(6)} %copy.11.refs_0_, s32[2,6]{1,0:T(2,128)} %bitcast.4, bf16[2,6]{1,0:T(2,128)(2,1)} %bitcast.6, bf16[6,3,32,512]{3,2,1,0:T(8,128)(2,1)} %refs_3_.1, bf16[3,32,512]{2,1,0:T(8,128)(2,1)} %refs_4_.1, s32[1,6]{1,0:T(1,128)} %bitcast.7, ...), custom_call_target="tpu_custom_call" | custom-call | tf_op jit(solution)/shard_map/coadd/pallas_call | solution.py:531
  18.1 0.7 %leave.1 = (bf16[3,32,256]{2,1,0:T(8,128)(2,1)}, bf16[3,32,256]{2,1,0:T(8,128)(2,1)}) custom-call(bf16[3,32,256]{2,1,0:T(8,128)(2,1)S(1)} %get-tuple-element.4.coadd_in, bf16[3,32,256]{2,1,0:T(8,128)(2,1)S(1)} %get-tuple-element.5.depth_in), custom_call_target="tpu_custom_call" | custom-call | tf_op jit(solution)/shard_map/leave/pallas_call | solution.py:579

commit v4 on v3

--- a/solution.py
+++ b/solution.py
@@ -16,7 +16,7 @@
 CAPACITY = 2
 CLIP_WIDTH = 3.0
 NOBODY = -64.0
-PRIOR_LANE = 64
+PRIOR_PARTS = 3
 AT_ONCE = 4
 TILE, DY, DX, FY, FX, SIGMA = range(6)
 MESH = pl.DeviceIdType.MESH
@@ -57,7 +57,7 @@
     (
         coadd_ref, depth_ref,
         offset_ref, frac_ref, template_ref, tile_ref, sigma_ref, mask_ref, prior_ref,
-        pixels, small, group, others, tap_table, lag_ref, kernel_x, columns, columns_held, template_held,
+        pixels, small, group, relay, others, tap_table, lag_ref, kernel_x, columns, columns_held, template_held,
         framed, flux, left, weigh, inverse, send, held, cover_ref,
         local_sem, message_sem, template_sem, columns_sem, flux_sem, sent_sem,
     ) = refs[9:]
@@ -104,7 +104,7 @@
     halves = 2 if part % (2 * LANES) == 0 else 1
     chunks = []
     for b in range(bands):
-        pieces = halves if b in (0, bands - 1) else 1
+        pieces = 1
         chunks += [(b, i * (part // pieces), part // pieces) for i in range(pieces)]
 
     tall = (2 * LANES, LANES)
@@ -180,10 +180,10 @@
                 sent_sem.at[1], template_sem.at[b], {"sky": sky_peer(d)},
             )
 
+    over_slots(build_kernel)
     for load in loads[2:8]:
         load.wait()
 
-    over_slots(build_kernel)
     warp_columns(0)
     lane = iota((8, LANES), 1)
     small[...] = jnp.ones_like(small)
@@ -218,9 +218,12 @@
     prior = jnp.sum(prior, 1, keepdims=True)
     high = rounded(prior)
     middle = rounded(prior - high)
-    by_lane = jnp.where(lane == PRIOR_LANE, high, by_lane)
-    by_lane = jnp.where(lane == PRIOR_LANE + 1, middle, by_lane)
-    by_lane = jnp.where(lane == PRIOR_LANE + 2, prior - high - middle, by_lane)
+    prior_at = field_at + fields
+    parts = jnp.where(lane == prior_at, high, 0.0) + jnp.where(lane == prior_at + 1, middle, 0.0)
+    parts = parts + jnp.where(lane == prior_at + 2, prior - high - middle, 0.0)
+    if held_slots > 8:
+        parts = jnp.concatenate([parts, jnp.zeros((held_slots - 8, LANES), F32)], 0)
+    by_slot = jnp.where(iota(by_slot.shape, 1) < prior_at, by_slot, parts)
     group[0] = jnp.concatenate([by_slot, by_lane], 0).astype(BF16)
 
     def column(a, f):
@@ -242,8 +245,9 @@
 
     for d in range(1, epochs):
         remote(group.at[0], group.at[d], sent_sem.at[2], message_sem.at[0], {"epoch": epoch_peer(d)})
-    for i in range(halves):
-        send_columns(i)
+    for i, chunk in enumerate(chunks):
+        if chunk[0] == 0:
+            send_columns(i)
     send_template(0)
     for b in range(1, bands):
 
@@ -362,8 +366,9 @@
 
     def meet_epoch_peers():
         wait_bytes(group.at[1:], message_sem.at[0])
+        relay[...] = jnp.concatenate([group[d, :held_slots] for d in range(epochs)], 0)
         for d in range(1, sky):
-            remote(group, others.at[d - 1], sent_sem.at[3], message_sem.at[1], {"sky": sky_peer(d)})
+            remote(relay, others.at[d - 1], sent_sem.at[3], message_sem.at[1], {"sky": sky_peer(d)})
         if sky == at_once:
 
             for d in range(1, epochs):
@@ -379,8 +384,6 @@
             for d in range(1, sky):
                 at = pl.ds(pl.multiple_of(MARGIN + lax.rem(me - d + sky, sky) * rows, 8), rows)
                 framed[b, at] = template_held[d - 1, b].astype(F32)
-        if i == 0:
-            pl.when(near_core)(send_held_back)
         for d in range(epochs):
             if d == 1:
 
@@ -392,6 +395,8 @@
                 process(d, chunk, first_owner)
 
             all_owners(step)
+        if i == 0:
+            pl.when(near_core)(send_held_back)
 
         for d in range(1, sky):
             at = pl.ds(pl.multiple_of(MARGIN + sky_peer(d) * rows, 8), rows)
@@ -416,12 +421,11 @@
     to_cols = ones_where(to_cols)
 
     def depth_from(groups):
-        messages = [message[e] for message in groups for e in range(epochs)]
-        every = jnp.concatenate([m[:held_slots].astype(F32) for m in messages], 0)
+        every = jnp.concatenate([message.astype(F32) for message in groups], 0)
         prior_total = jnp.zeros((8, 1), F32)
-        for message in messages[::epochs]:
-            message = message[held_slots : held_slots + 8].astype(F32)
-            prior_total = prior_total + jnp.sum(message[:, PRIOR_LANE : PRIOR_LANE + 3], 1, keepdims=True)
+        for message in groups:
+            prior = message[:8].astype(F32)[:, prior_at : prior_at + PRIOR_PARTS]
+            prior_total = prior_total + jnp.sum(prior, 1, keepdims=True)
         number = every.shape[0]
         taps = slot_taps(every)
         cover = cover_ref.at[:number]
@@ -470,12 +474,12 @@
         return (dot_first(lhs, cells), *totals)
 
     if sky <= AT_ONCE:
-        weights, *totals = depth_from([group[...]] + [others[d - 1] for d in range(1, sky)])
+        weights, *totals = depth_from([relay[...]] + [others[d - 1] for d in range(1, sky)])
     else:
         weights, *totals = lax.fori_loop(
             0, sky - 1,
             lambda d, sums: tuple(x + y for x, y in zip(sums, depth_from([others[d]]))),
-            depth_from([group[...]]),
+            depth_from([relay[...]]),
         )
     means = [total * (1.0 / (sky * rows * cols)) for total in totals]
     diagonal = iota((rows, rows), 0) == iota((rows, rows), 1)
@@ -544,7 +548,8 @@
             pltpu.VMEM((bands, slots, rows, cols), BF16),
             pltpu.VMEM((field_rows, LANES), F32),
             pltpu.VMEM((epochs, message, LANES), BF16),
-            pltpu.VMEM((sky - 1, epochs, message, LANES), BF16),
+            pltpu.VMEM((epochs * held_slots, LANES), BF16),
+            pltpu.VMEM((sky - 1, epochs * held_slots, LANES), BF16),
             pltpu.VMEM((2, slots, 8, LANES), F32),
             pltpu.VMEM((2 * LANES, LANES), F32),
             pltpu.VMEM((slots, 2 * LANES, LANES), BF16),

time: 19 us -> 18.5 us (0.974)
  Pallas kernels: 17.5 us -> 17 us
    pallas_call x1, Pallas kernels: 16.9 us -> 16.4 us  [on_device(): pl.pallas_call(functools.partial(coadd_kernel, (bands, sky, epochs, rows,...]
where the time goes in v4:
time: 18.5 us; the launch traced here: 18.3 us
  Pallas kernels  17 us (92%)
  between operations  1.29 us (7%)
    pallas_call x1, Pallas kernels, on_device(): pl.pallas_call(functools.partial(coadd_kernel, (bands, sky, epochs, rows,...  16.4 us
    pallas_call x1, Pallas kernels, on_device(): pl.pallas_call(leave_kernel, out_shape=(block, block), in_specs=[vmem] *...  0.66 us

profile of v4, /device:TPU:0, one launch (start us, length us, event | category | flops | bytes accessed | tf_op | source)
XLA Modules:
  0.0 18.3 jit_solution(5038082493261857933)
XLA Ops:
  1.3 16.4 %coadd.1 = (bf16[3,32,256]{2,1,0:T(8,128)(2,1)S(1)}, bf16[3,32,256]{2,1,0:T(8,128)(2,1)S(1)}) custom-call(s32[1]{0:T(128)S(6)} %copy.11.refs_0_, s32[2,6]{1,0:T(2,128)} %bitcast.4, bf16[2,6]{1,0:T(2,128)(2,1)} %bitcast.6, bf16[6,3,32,512]{3,2,1,0:T(8,128)(2,1)} %refs_3_.1, bf16[3,32,512]{2,1,0:T(8,128)(2,1)} %refs_4_.1, s32[1,6]{1,0:T(1,128)} %bitcast.7, ...), custom_call_target="tpu_custom_call" | custom-call | tf_op jit(solution)/shard_map/coadd/pallas_call | solution.py:535
  17.7 0.7 %leave.1 = (bf16[3,32,256]{2,1,0:T(8,128)(2,1)}, bf16[3,32,256]{2,1,0:T(8,128)(2,1)}) custom-call(bf16[3,32,256]{2,1,0:T(8,128)(2,1)S(1)} %get-tuple-element.4.coadd_in, bf16[3,32,256]{2,1,0:T(8,128)(2,1)S(1)} %get-tuple-element.5.depth_in), custom_call_target="tpu_custom_call" | custom-call | tf_op jit(solution)/shard_map/leave/pallas_call | solution.py:584

commit v5 on v4

--- a/solution.py
+++ b/solution.py
@@ -77,6 +77,8 @@
     def sky_peer(d):
         return lax.rem(me + d, sky)
 
+    far_order = [jnp.where(me < sky // 2, sky - k, k) for k in range(1, sky)]
+
     def epoch_peer(d):
         return lax.rem(epoch + d, epochs)
 
@@ -90,7 +92,8 @@
     sources = inputs[:2] + [inputs[2].at[:, 0]] + inputs[3:] + [inputs[2].at[:, b] for b in range(1, bands)]
     loads = []
     for i, (source, target) in enumerate(zip(sources, targets)):
-        loads.append(pltpu.make_async_copy(source, target, local_sem.at[i]))
+        sem = sent_sem.at[i] if i < 5 else local_sem.at[i - 5]
+        loads.append(pltpu.make_async_copy(source, target, sem))
         loads[-1].start()
 
     def remote(src, dst, sent, received, where):
@@ -104,7 +107,7 @@
     halves = 2 if part % (2 * LANES) == 0 else 1
     chunks = []
     for b in range(bands):
-        pieces = 1
+        pieces = halves if b == bands - 1 else 1
         chunks += [(b, i * (part // pieces), part // pieces) for i in range(pieces)]
 
     tall = (2 * LANES, LANES)
@@ -359,9 +362,9 @@
     if sky == at_once:
         prepare(0, 0)
 
-    def send_held_back():
+    def send_held_back(bands_of):
         for i, chunk in enumerate(chunks):
-            if chunk[0] > 0:
+            if chunk[0] in bands_of:
                 send_columns_now(i)
 
     def meet_epoch_peers():
@@ -386,6 +389,8 @@
                 framed[b, at] = template_held[d - 1, b].astype(F32)
         for d in range(epochs):
             if d == 1:
+                if i == 1:
+                    pl.when(near_core)(functools.partial(send_held_back, range(2, bands)))
 
                 wait_bytes(columns_held.at[:, b, :, pl.ds(first, width)], columns_sem.at[i])
 
@@ -396,12 +401,12 @@
 
             all_owners(step)
         if i == 0:
-            pl.when(near_core)(send_held_back)
+            pl.when(near_core)(functools.partial(send_held_back, (1,)))
 
         for d in range(1, sky):
             at = pl.ds(pl.multiple_of(MARGIN + sky_peer(d) * rows, 8), rows)
             send[d - 1, b, :, lanes] = flux[b, at, lanes].astype(BF16)
-        for d in range(1, sky):
+        for d in far_order:
             at = pl.ds(first, width)
             remote(
                 send.at[d - 1, b, :, at], held.at[d - 1, b, :, at],
@@ -564,11 +569,11 @@
             pltpu.VMEM((sky - 1, bands, rows, part), BF16),
             pltpu.VMEM((sky - 1, bands, rows, part), BF16),
             pltpu.VMEM(((sky if sky <= AT_ONCE else 1) * epochs * held_slots, cols), F32),
-            pltpu.SemaphoreType.DMA((bands + 7,)),
+            pltpu.SemaphoreType.DMA((bands + 2,)),
             pltpu.SemaphoreType.DMA((2,)),
             pltpu.SemaphoreType.DMA((bands,)),
-            pltpu.SemaphoreType.DMA((bands + 2,)),
-            pltpu.SemaphoreType.DMA((bands + 2,)),
+            pltpu.SemaphoreType.DMA((bands + 1,)),
+            pltpu.SemaphoreType.DMA((bands + 1,)),
             pltpu.SemaphoreType.DMA((5,)),
         ],
         compiler_params=pltpu.CompilerParams(collective_id=0, has_side_effects=True, vmem_limit_bytes=limit),

time: 18.5 us -> 18.3 us (0.989)
  Pallas kernels: 17 us -> 16.8 us
    pallas_call x1, Pallas kernels: 16.4 us -> 16.2 us  [on_device(): pl.pallas_call(functools.partial(coadd_kernel, (bands, sky, epochs, rows,...]
where the time goes in v5:
time: 18.3 us; the launch traced here: 18.1 us
  Pallas kernels  16.8 us (92%)
  between operations  1.29 us (7%)
    pallas_call x1, Pallas kernels, on_device(): pl.pallas_call(functools.partial(coadd_kernel, (bands, sky, epochs, rows,...  16.2 us
    pallas_call x1, Pallas kernels, on_device(): pl.pallas_call(leave_kernel, out_shape=(block, block), in_specs=[vmem] *...  0.66 us

profile of v5, /device:TPU:0, one launch (start us, length us, event | category | flops | bytes accessed | tf_op | source)
XLA Modules:
  0.0 18.1 jit_solution(122011814985229902)
XLA Ops:
  1.3 16.2 %coadd.1 = (bf16[3,32,256]{2,1,0:T(8,128)(2,1)S(1)}, bf16[3,32,256]{2,1,0:T(8,128)(2,1)S(1)}) custom-call(s32[1]{0:T(128)S(6)} %copy.11.refs_0_, s32[2,6]{1,0:T(2,128)} %bitcast.4, bf16[2,6]{1,0:T(2,128)(2,1)} %bitcast.6, bf16[6,3,32,512]{3,2,1,0:T(8,128)(2,1)} %refs_3_.1, bf16[3,32,512]{2,1,0:T(8,128)(2,1)} %refs_4_.1, s32[1,6]{1,0:T(1,128)} %bitcast.7, ...), custom_call_target="tpu_custom_call" | custom-call | tf_op jit(solution)/shard_map/coadd/pallas_call | solution.py:540
  17.4 0.7 %leave.1 = (bf16[3,32,256]{2,1,0:T(8,128)(2,1)}, bf16[3,32,256]{2,1,0:T(8,128)(2,1)}) custom-call(bf16[3,32,256]{2,1,0:T(8,128)(2,1)S(1)} %get-tuple-element.4.coadd_in, bf16[3,32,256]{2,1,0:T(8,128)(2,1)S(1)} %get-tuple-element.5.depth_in), custom_call_target="tpu_custom_call" | custom-call | tf_op jit(solution)/shard_map/leave/pallas_call | solution.py:589
